TPU v7x, 32 devices: a whole 2x2x4 slice. The times are simulated.
32 devices in a mesh: gx: 4 (over y, core), gy: 8 (over z, x).
Axes of the slice: x: 2, y: 2, z: 4, core: 2. Of those that a mesh axis runs over, the one named last changes fastest.
Arguments:
- tokens: bfloat16 [256, 4096], P('gy', 'gx'), may hold values from -140 to 140
- cotangent: bfloat16 [256, 4096], P('gy', 'gx'), may hold values from -6 to 6
- gate_weight: bfloat16 [4096, 14336], P('gx', 'gy'), may hold values from -5 to 5
- up_weight: bfloat16 [4096, 14336], P('gx', 'gy'), may hold values from -5 to 5
- down_weight: bfloat16 [14336, 4096], P('gy', 'gx'), may hold values from -5 to 5
Outputs:
- output: bfloat16 [256, 4096], P('gy', 'gx')
- input_grad: bfloat16 [256, 4096], P('gy', 'gx')
- gate_grad: bfloat16 [4096, 14336], P('gx', 'gy')
- up_grad: bfloat16 [4096, 14336], P('gx', 'gy')
- down_grad: bfloat16 [14336, 4096], P('gy', 'gx')
All inputs are finite; a program needn't handle non-finite values.
Results may differ from a plain program's by a relative error of at most 0.005.
The roundings to bfloat16 on the way count: a program that leaves them out, or rounds other values in their place, can miss the bound.
Values may be sent and summed in bfloat16 or wider, within the bound.
A program may use at most 128 MiB of HBM per device.

v0:
```python
import jax
import jax.numpy as jnp
from jax import lax
from jax.sharding import PartitionSpec as P

ROT_BLOCK = 128
HID_BLOCK = 64


fp_top = 448.0
tiny = 1e-06


def hadamard_table(block_size):
    row_ids = jnp.arange(block_size, dtype=jnp.int32)[:, None]
    col_ids = jnp.arange(block_size, dtype=jnp.int32)[None, :]
    shared = row_ids & col_ids
    parity = jnp.zeros((block_size, block_size), jnp.int32)
    for bit_pos in range(max(block_size.bit_length() - 1, 1)):
        parity = parity + (shared >> bit_pos & 1)
    return (1 - 2 * (parity % 2)).astype(jnp.float32)


def rotate_cols(matrix, block_size):
    row_total, col_total = matrix.shape
    table = hadamard_table(block_size)
    blocks = matrix.reshape(row_total, col_total // block_size, block_size)
    if matrix.dtype == jnp.bfloat16:
        turned = jnp.einsum(
            "rbk,kl->rbl", blocks, table.astype(jnp.bfloat16), preferred_element_type=jnp.float32
        )
    else:
        turned = jnp.einsum("rbk,kl->rbl", blocks, table, precision=lax.Precision.HIGHEST)
    return turned.reshape(row_total, col_total) * block_size ** (-0.5)


def rotate_rows(matrix, block_size):
    row_total, col_total = matrix.shape
    table = hadamard_table(block_size)
    blocks = matrix.reshape(row_total // block_size, block_size, col_total)
    if matrix.dtype == jnp.bfloat16:
        turned = jnp.einsum(
            "kl,bkc->blc", table.astype(jnp.bfloat16), blocks, preferred_element_type=jnp.float32
        )
    else:
        turned = jnp.einsum("kl,bkc->blc", table, blocks, precision=lax.Precision.HIGHEST)
    return turned.reshape(row_total, col_total) * block_size ** (-0.5)


def soft_cast(values, top):
    return (fp_top * jnp.tanh(values / (top + tiny))).astype(jnp.bfloat16)


def peak(values):
    return jnp.max(jnp.abs(values))


def contract_rows(left_mat, right_mat):
    return lax.dot_general(
        left_mat, right_mat, (((0,), (0,)), ((), ())), preferred_element_type=jnp.float32
    )


def contract_cols(left_mat, right_mat):
    return lax.dot_general(
        left_mat, right_mat, (((1,), (1,)), ((), ())), preferred_element_type=jnp.float32
    )


def shards(tokens, cotangent, gate_weight, up_weight, down_weight):
    gate_rot = rotate_rows(gate_weight, ROT_BLOCK)
    up_rot = rotate_rows(up_weight, ROT_BLOCK)
    down_rot = rotate_rows(down_weight, HID_BLOCK)
    gate_peak, up_peak, down_peak = lax.pmax(
        (peak(gate_rot), peak(up_rot), peak(down_rot)), ("gx", "gy")
    )
    gate_cast = soft_cast(gate_rot, gate_peak)
    up_cast = soft_cast(up_rot, up_peak)
    down_cast = soft_cast(down_rot, down_peak)
    hid_width = gate_weight.shape[1]
    token_rot = rotate_cols(tokens, ROT_BLOCK)
    token_peak = lax.pmax(peak(token_rot), ("gx", "gy"))
    token_cast = lax.all_gather(soft_cast(token_rot, token_peak), "gy", axis=0, tiled=True)
    weight_pair = jnp.concatenate([gate_cast, up_cast], axis=1)
    picked = token_cast
    paired = lax.psum_scatter(
        jnp.dot(picked, weight_pair, preferred_element_type=jnp.float32),
        "gx",
        scatter_dimension=0,
        tiled=True,
    )
    gate_pre = paired[:, :hid_width] * (token_peak * gate_peak / (fp_top * fp_top))
    up_pre = paired[:, hid_width:] * (token_peak * up_peak / (fp_top * fp_top))
    hidden = (jax.nn.silu(gate_pre) * up_pre).astype(jnp.bfloat16)
    hidden_rot = rotate_cols(hidden, HID_BLOCK)
    hidden_peak = lax.pmax(peak(hidden_rot), ("gx", "gy"))
    hidden_cast = lax.all_gather(soft_cast(hidden_rot, hidden_peak), "gx", axis=0, tiled=True)
    picked = hidden_cast
    out_sum = lax.psum_scatter(
        jnp.dot(picked, down_cast, preferred_element_type=jnp.float32),
        "gy",
        scatter_dimension=0,
        tiled=True,
    )
    output = (out_sum * (hidden_peak * down_peak / (fp_top * fp_top))).astype(jnp.bfloat16)
    all_cot = lax.all_gather(cotangent, "gy", axis=0, tiled=True)
    down_grad = rotate_rows(
        contract_rows(hidden_cast, all_cot) * (hidden_peak / fp_top), HID_BLOCK
    ).astype(jnp.bfloat16)
    picked = all_cot
    back_sum = lax.psum_scatter(
        contract_cols(picked, down_cast), "gx", scatter_dimension=0, tiled=True
    )
    hidden_grad = rotate_cols(back_sum * (down_peak / fp_top), HID_BLOCK)
    sigmoid_gate = jax.nn.sigmoid(gate_pre)
    gate_act = (
        hidden_grad * up_pre * sigmoid_gate * (1.0 + gate_pre * (1.0 - sigmoid_gate))
    ).astype(jnp.bfloat16)
    up_act = (hidden_grad * gate_pre * sigmoid_gate).astype(jnp.bfloat16)
    all_gate_act, all_up_act = (
        lax.all_gather(gate_act, "gx", axis=0, tiled=True),
        lax.all_gather(up_act, "gx", axis=0, tiled=True),
    )
    gate_grad = rotate_rows(
        contract_rows(token_cast, all_gate_act) * (token_peak / fp_top), ROT_BLOCK
    ).astype(jnp.bfloat16)
    up_grad = rotate_rows(
        contract_rows(token_cast, all_up_act) * (token_peak / fp_top), ROT_BLOCK
    ).astype(jnp.bfloat16)
    input_sum = lax.psum_scatter(
        contract_cols(all_gate_act, gate_cast) * (gate_peak / fp_top)
        + contract_cols(all_up_act, up_cast) * (up_peak / fp_top),
        "gy",
        scatter_dimension=0,
        tiled=True,
    )
    input_grad = rotate_cols(input_sum, ROT_BLOCK).astype(jnp.bfloat16)
    return (output, input_grad, gate_grad, up_grad, down_grad)


def solution(mesh):
    in_specs = (P("gy", "gx"), P("gy", "gx"), P("gx", "gy"), P("gx", "gy"), P("gy", "gx"))
    out_specs = (P("gy", "gx"), P("gy", "gx"), P("gx", "gy"), P("gx", "gy"), P("gy", "gx"))
    return jax.shard_map(shards, mesh=mesh, in_specs=in_specs, out_specs=out_specs, check_vma=False)
```

profile of v0, /device:TPU:0, one launch (start us, length us, event | category | flops | bytes accessed | tf_op | source)
XLA Modules:
  0.0 379.1 jit_solution(8001831813268286544)
XLA Ops:
  8.8 7.0 %abs_reduce_fusion.1 = (f32[]{:T(128)}, f32[128,8,1792]{2,0,1:T(8,128)}) fusion(bf16[8,128,1792]{2,1,0:T(8,128)(2,1)} %bitcast.114), kind=kOutput, calls=%fused_computation.11 | convolution fusion | flops 475856896 | bytes 11010052 | tf_op jit(solution)/shard_map/kl,bkc->blc/dot_general | solution.py:42
  15.9 4.8 %abs_reduce_fusion.2 = (f32[]{:T(128)}, f32[128,8,1792]{2,0,1:T(8,128)}) fusion(bf16[8,128,1792]{2,1,0:T(8,128)(2,1)S(1)} %bitcast.115), kind=kOutput, calls=%fused_computation.12 | convolution fusion | flops 475856896 | bytes 11010052 | tf_op jit(solution)/shard_map/kl,bkc->blc/dot_general | solution.py:42
  20.6 42.3 %all-reduce.1 = (f32[]{:T(128)}, f32[]{:T(128)}, f32[]{:T(128)}) all-reduce(f32[]{:T(128)} %get-tuple-element.12, f32[]{:T(128)} %get-tuple-element.14, f32[]{:T(128)} %get-tuple-element.16), channel_id=1, replica_groups=mesh['gx'=4,'gy'=8] {'gx','gy'}, use_global_device_ids=true, to_apply=%region_1.2 | all-reduce | flops 3 | bytes 24 | tf_op jit(solution)/shard_map/pmax | solution.py:82
  63.6 31.4 %all_gather.15 = bf16[256,1024]{1,0:T(8,128)(2,1)S(1)} all-gather(bf16[32,1024]{1,0:T(8,128)(2,1)S(1)} %copy_bitcast_fusion.1), channel_id=1, replica_groups=mesh['gx'=4,'gy'=8] {'gy'}, dimensions={0}, use_global_device_ids=true | all-gather | bytes 589824 | tf_op jit(solution)/shard_map/all_gather | solution.py:83
  96.2 4.4 %multiply_convert_fusion.1 = bf16[128,8,1792]{2,0,1:T(8,128)(2,1)S(1)} fusion(f32[128,8,1792]{2,0,1:T(8,128)} %get-tuple-element.15, f32[]{:T(128)S(6)} %add.255), kind=kLoop, calls=%fused_computation.5 | loop fusion | flops 7340032 | bytes 11010052 | tf_op jit(solution)/shard_map/convert.2
  102.6 1.8 copy-done.6
  104.4 4.9 %fusion = f32[256,3584]{1,0:T(8,128)} fusion(bf16[256,1024]{1,0:T(8,128)(2,1)S(1)} %all_gather.15, bf16[1024,1792]{1,0:T(8,128)(2,1)S(1)} %bitcast.117, bf16[1024,1792]{1,0:T(8,128)(2,1)S(1)} %bitcast.119), kind=kOutput, calls=%fused_computation | convolution fusion | flops 1893728256 | bytes 11534336 | tf_op jit(solution)/shard_map/dot_general | solution.py:87
  112.0 31.6 %all_gather.17 = bf16[256,1024]{1,0:T(8,128)(2,1)S(1)} all-gather(bf16[32,1024]{1,0:T(8,128)(2,1)S(1)} %copy-done.9), channel_id=1, replica_groups=mesh['gx'=4,'gy'=8] {'gy'}, dimensions={0}, use_global_device_ids=true | all-gather | bytes 589824 | tf_op jit(solution)/shard_map/all_gather | solution.py:106
  143.6 6.8 %abs_reduce_fusion = (f32[]{:T(128)}, f32[64,28,1024]{2,0,1:T(8,128)}) fusion(bf16[28,64,1024]{2,1,0:T(8,128)(2,1)} %bitcast.116), kind=kOutput, calls=%fused_computation.10 | convolution fusion | flops 240521216 | bytes 11010052 | tf_op jit(solution)/shard_map/kl,bkc->blc/dot_general | solution.py:42
  150.7 1.3 multiply_convert_fusion.9
  153.5 39.7 %all-reduce = (f32[]{:T(128)}, f32[]{:T(128)}) all-reduce(f32[]{:T(128)} %get-tuple-element.18, f32[]{:T(128)} %get-tuple-element.20), channel_id=1, replica_groups=mesh['gx'=4,'gy'=8] {'gx','gy'}, use_global_device_ids=true, to_apply=%region_8.9 | all-reduce | flops 2 | bytes 16 | tf_op jit(solution)/shard_map/pmax | solution.py:96
  193.9 4.3 %multiply_convert_fusion = bf16[64,28,1024]{2,0,1:T(8,128)(2,1)S(1)} fusion(f32[64,28,1024]{2,0,1:T(8,128)} %get-tuple-element.21, f32[]{:T(128)S(6)} %add.264), kind=kLoop, calls=%fused_computation.4 | loop fusion | flops 7340032 | bytes 11010052 | tf_op jit(solution)/shard_map/convert
  198.2 1.8 copy-done.8
  200.1 2.4 convolution_bitcast_fusion
  202.4 2.8 copy.47
  211.2 10.4 %all_gather.16 = bf16[256,1792]{1,0:T(8,128)(2,1)S(1)} all-gather(bf16[64,1792]{1,0:T(8,128)(2,1)S(1)} %mul.236), channel_id=1, replica_groups=mesh['gx'=4,'gy'=8] {'gx'}, dimensions={0}, use_global_device_ids=true | all-gather | bytes 1146880 | tf_op jit(solution)/shard_map/all_gather | solution.py:97
  221.5 4.4 %fusion.110 = f32[256,1024]{1,0:T(8,128)} fusion(bf16[256,1792]{1,0:T(8,128)(2,1)S(1)} %all_gather.16, bf16[1792,1024]{1,0:T(8,128)(2,1)} %bitcast.122), kind=kOutput, calls=%fused_computation.139 | convolution fusion | flops 939524096 | bytes 5636096 | tf_op jit(solution)/shard_map/dot_general | solution.py:100
  226.0 1.1 convolution_multiply_fusion
  227.1 8.5 %multiply_convert_fusion.3 = bf16[28,1024,64]{1,2,0:T(8,128)(2,1)} fusion(f32[28,64,1024]{2,1,0:T(8,128)S(1)} %bitcast.110), kind=kOutput, calls=%fused_computation.7 | convolution fusion | flops 1413087232 | bytes 11010048 | tf_op jit(solution)/shard_map/kl,bkc->blc/dot_general | solution.py:46
  236.0 1.3 copy.48
  237.4 1.6 convolution_multiply_fusion.5
  240.2 9.5 %all_gather.19 = bf16[256,1792]{1,0:T(8,128)(2,1)S(1)} all-gather(bf16[64,1792]{1,0:T(8,128)(2,1)S(1)} %get-tuple-element.11), channel_id=1, replica_groups=mesh['gx'=4,'gy'=8] {'gx'}, dimensions={0}, use_global_device_ids=true | all-gather | bytes 1146880 | tf_op jit(solution)/shard_map/all_gather | solution.py:122
  249.7 9.4 %all_gather.18 = bf16[256,1792]{1,0:T(8,128)(2,1)S(1)} all-gather(bf16[64,1792]{1,0:T(8,128)(2,1)S(1)} %get-tuple-element.10), channel_id=1, replica_groups=mesh['gx'=4,'gy'=8] {'gx'}, dimensions={0}, use_global_device_ids=true | all-gather | bytes 1146880 | tf_op jit(solution)/shard_map/all_gather | solution.py:121
  259.1 3.2 convolution_multiply_fusion.3
  262.3 2.1 fusion.4
  264.5 39.1 %reduce-scatter.9.cloned.1.call-done = f32[32,1024]{1,0:T(8,128)} async-done(((f32[256,1024]{1,0:T(8,128)}), f32[32,1024]{1,0:T(8,128)}) %reduce-scatter.9.cloned.1.call-update) | async-done | bytes 131088 | tf_op jit(solution)/shard_map/reduce_scatter | solution.py:99
  303.6 1.5 multiply_convert_fusion.11
  305.1 1.2 convolution_multiply_fusion.2
  306.3 1.2 convolution_multiply_fusion.1
  307.5 9.0 %multiply_convert_fusion.5 = bf16[8,1792,128]{1,2,0:T(8,128)(2,1)} fusion(f32[8,128,1792]{2,1,0:T(8,128)S(1)} %bitcast.111), kind=kOutput, calls=%fused_computation.9 | convolution fusion | flops 2822815744 | bytes 11010048 | tf_op jit(solution)/shard_map/kl,bkc->blc/dot_general | solution.py:46
  316.5 8.7 %multiply_convert_fusion.4 = bf16[8,1792,128]{1,2,0:T(8,128)(2,1)} fusion(f32[8,128,1792]{2,1,0:T(8,128)S(1)} %bitcast.112), kind=kOutput, calls=%fused_computation.8 | convolution fusion | flops 2822815744 | bytes 11010048 | tf_op jit(solution)/shard_map/kl,bkc->blc/dot_general | solution.py:46
  325.3 45.3 %reduce-scatter.11.cloned.1.call-done = f32[32,1024]{1,0:T(8,128)} async-done(((f32[256,1024]{1,0:T(8,128)}), f32[32,1024]{1,0:T(8,128)}) %reduce-scatter.11.cloned.1.call-update) | async-done | bytes 131088 | tf_op jit(solution)/shard_map/reduce_scatter | solution.py:130
  (43 shorter events, 9.9 us)
Async XLA Ops:
  7.2 0.8 copy-start
  7.2 143.5 %reduce-scatter.7.cloned.1.call-start = ((), (), s32[]{:S(2)}) async-start(), calls=%async_computation.4 | async-start | bytes 4587520 | tf_op jit(solution)/shard_map/reduce_scatter | solution.py:86
  8.0 7.9 %copy-start.4 = (bf16[1024,1792]{1,0:T(8,128)(2,1)S(1)}, bf16[1024,1792]{1,0:T(8,128)(2,1)}, u32[]{:S(2)}) copy-start(bf16[1024,1792]{1,0:T(8,128)(2,1)} %param.7) | copy-start | bytes 11010052
  96.2 5.2 %copy-start.2 = (f32[128,8,1792]{2,0,1:T(8,128)S(1)}, f32[128,8,1792]{2,0,1:T(8,128)}, u32[]{:S(2)}) copy-start(f32[128,8,1792]{2,0,1:T(8,128)} %get-tuple-element.17) | copy-start | bytes 22020100
  100.6 1.9 copy-start.5
  102.5 1.8 copy-start.6
  104.4 7.6 %copy-start.9 = (bf16[32,1024]{1,0:T(8,128)(2,1)S(1)}, bf16[32,1024]{1,0:T(8,128)(2,1)}, u32[]{:S(2)}) copy-start(bf16[32,1024]{1,0:T(8,128)(2,1)} %param.6) | copy-start | bytes 196612
  109.3 126.7 %reduce-scatter.13.cloned.1.call-start = ((), (), s32[]{:S(2)}) async-start(), calls=%async_computation.7 | async-start | bytes 2293760
  198.2 1.8 copy-start.8
  205.2 98.4 %reduce-scatter.9.cloned.1.call-start = ((), (), s32[]{:S(2)}) async-start(), calls=%async_computation.5 | async-start | bytes 1179648 | tf_op jit(solution)/shard_map/reduce_scatter | solution.py:99
  235.6 4.3 %copy-start.3 = (f32[64,3584]{1,0:T(8,128)S(1)}, f32[64,3584]{1,0:T(8,128)}, u32[]{:S(2)}) copy-start(f32[64,3584]{1,0:T(8,128)} %reduce-scatter.7.cloned.1.call-done) | copy-start | bytes 2752516
  235.6 135.0 %reduce-scatter.11.cloned.1.call-start = ((), (), s32[]{:S(2)}) async-start(), calls=%async_computation.6 | async-start | bytes 1179648 | tf_op jit(solution)/shard_map/reduce_scatter | solution.py:130
  239.9 22.4 %copy-start.7 = (bf16[128,8,1792]{2,0,1:T(8,128)(2,1)S(1)}, bf16[128,8,1792]{2,0,1:T(8,128)(2,1)}, u32[]{:S(2)}) copy-start(bf16[128,8,1792]{2,0,1:T(8,128)(2,1)} %copy-done.6) | copy-start | bytes 11010052
  307.5 65.0 %copy-start.1 = (bf16[32,1024]{1,0:T(8,128)(2,1)S(1)}, bf16[32,1024]{1,0:T(8,128)(2,1)}, u32[]{:S(2)}) copy-start(bf16[32,1024]{1,0:T(8,128)(2,1)} %param.5) | copy-start | bytes 196612
Sparse Core Ops, SparseCore 0:
  109.4 41.1 reduce-scatter.6
  205.3 30.6 reduce-scatter.12
  239.4 64.1 reduce-scatter.8
  306.9 63.7 reduce-scatter.10
where the time goes:
time: 380 us; the launch traced here: 379 us
  blocking collectives  174 us (46%)
  waiting for transfers between devices  84.9 us (22%)
  matrix products  69.2 us (18%)
  between operations  24.2 us (6%)
  other arithmetic  13.1 us (3%)
  local copies, waits for them, and re-layouts  13 us (3%)
    reduce_scatter x1, waiting for transfers between devices, shards(): lax.psum_scatter(contract_cols(all_gate_act, gate_cast) * (gate_peak / fp...  45.3 us
    pmax x1, blocking collectives, shards(): token_peak = lax.pmax(peak(token_rot), ('gx', 'gy'))  42.3 us
    pmax x1, blocking collectives, shards(): hidden_peak = lax.pmax(peak(hidden_rot), ('gx', 'gy'))  39.7 us
    reduce_scatter x1, waiting for transfers between devices, shards(): lax.psum_scatter(jnp.dot(picked, down_cast, preferred_element_type=jnp.fl...  39.1 us
    all_gather x1, blocking collectives, shards(): all_cot = lax.all_gather(cotangent, 'gy', axis=0, tiled=True)  31.6 us
    all_gather x1, blocking collectives, shards(): lax.all_gather(soft_cast(token_rot, token_peak), 'gy', axis=0, tiled=True)  31.4 us
    dot_general x3, matrix products, rotate_rows(): jnp.einsum('kl,bkc->blc', table, blocks, precision=lax.Precision.HIGHEST)  26.3 us
    dot_general x3, matrix products, rotate_rows(): jnp.einsum('kl,bkc->blc', table.astype(jnp.bfloat16), blocks, preferred_e...  18.6 us
  transfers between devices with their start and end apart: 4, of which 4 were waited for; matrix products, arithmetic and copies ran while one was open for 14% of the time, Pallas kernels for 0%

commit v1 on v0

v1 whole, which is shorter than its diff:
```python
import functools

import jax
import jax.numpy as jnp
from jax import lax
from jax.experimental import pallas as pl
from jax.experimental.pallas import tpu as pltpu
from jax.sharding import PartitionSpec as P

ROT_BLOCK = 128
HID_BLOCK = 64
CORES = 2

fp_top = 448.0
tiny = 1e-06

MESH = pl.DeviceIdType.MESH
VMEM = pl.BlockSpec(memory_space=pltpu.VMEM)
DMA = pltpu.SemaphoreType.DMA


def hadamard_table(block_size):
    row_ids = jnp.arange(block_size, dtype=jnp.int32)[:, None]
    col_ids = jnp.arange(block_size, dtype=jnp.int32)[None, :]
    shared = row_ids & col_ids
    parity = jnp.zeros((block_size, block_size), jnp.int32)
    for bit_pos in range(max(block_size.bit_length() - 1, 1)):
        parity = parity + (shared >> bit_pos & 1)
    return (1 - 2 * (parity % 2)).astype(jnp.float32)


def rotate_cols(matrix, block_size):
    row_total, col_total = matrix.shape
    table = hadamard_table(block_size)
    blocks = matrix.reshape(row_total, col_total // block_size, block_size)
    if matrix.dtype == jnp.bfloat16:
        turned = jnp.einsum(
            "rbk,kl->rbl", blocks, table.astype(jnp.bfloat16), preferred_element_type=jnp.float32
        )
    else:
        turned = jnp.einsum("rbk,kl->rbl", blocks, table, precision=lax.Precision.HIGHEST)
    return turned.reshape(row_total, col_total) * block_size ** (-0.5)


def rotate_rows(matrix, block_size):
    row_total, col_total = matrix.shape
    table = hadamard_table(block_size)
    blocks = matrix.reshape(row_total // block_size, block_size, col_total)
    turned = jnp.einsum(
        "kl,bkc->blc", table.astype(jnp.bfloat16), blocks, preferred_element_type=jnp.float32
    )
    return turned.reshape(row_total, col_total) * block_size ** (-0.5)


def soft_cast(values, top):
    return (fp_top * jnp.tanh(values / (top + tiny))).astype(jnp.bfloat16)


def peak(values):
    return jnp.max(jnp.abs(values))


def contract_rows(left_mat, right_mat):
    return lax.dot_general(
        left_mat, right_mat, (((0,), (0,)), ((), ())), preferred_element_type=jnp.float32
    )


def contract_cols(left_mat, right_mat):
    return lax.dot_general(
        left_mat, right_mat, (((1,), (1,)), ((), ())), preferred_element_type=jnp.float32
    )


def remote(src, dst, send, recv, target):
    return pltpu.make_async_remote_copy(
        src_ref=src, dst_ref=dst, send_sem=send, recv_sem=recv,
        device_id=target, device_id_type=MESH,
    )


def loop(low, high, body):
    def step(i, carry):
        body(i)
        return carry
    lax.fori_loop(low, high, step, 0)


def greet(n, me, axis):
    barrier = pltpu.get_barrier_semaphore()

    def hello(k):
        pl.semaphore_signal(
            barrier, inc=1, device_id={axis: lax.rem(me + k, n)}, device_id_type=MESH
        )

    loop(1, n, hello)


def exchange(n, me, axis, src, slots, send, recv):
    def copy(k, slot):
        return remote(
            src, slots.at[slot], send.at[k], recv.at[k], {axis: lax.rem(me + k, n)}
        )

    def start(k):
        copy(k, me).start()

    def finish(k):
        copy(k, lax.rem(me + n - k, n)).wait()

    return (lambda: loop(1, n, start)), (lambda: loop(1, n, finish))


def wide_gather_kernel(nx, ny, count, *refs):
    blocks, tile = refs[:count], refs[count]
    outs, tile_out = refs[count + 1 : 2 * count + 1], refs[2 * count + 1]
    slots_x, slots_y, mid, send, recv, sx, rx, sy, ry = refs[2 * count + 2 :]
    gx, gy = lax.axis_index("gx"), lax.axis_index("gy")
    greet(nx, gx, "gx")
    greet(ny, gy, "gy")
    pl.semaphore_wait(pltpu.get_barrier_semaphore(), nx - 1 + ny - 1)

    start_x, finish_x = exchange(nx, gx, "gx", tile, slots_x, sx, rx)
    start_y, finish_y = exchange(ny, gy, "gy", mid, slots_y, sy, ry)
    start_x()
    bulk = [
        exchange(ny, gy, "gy", blocks[i], outs[i], send.at[i], recv.at[i]) for i in range(count)
    ]
    slots_x[gx] = tile[...]
    for i in range(count):
        outs[i][gy] = blocks[i][...]
    finish_x()
    mid[...] = jnp.max(slots_x[...], axis=0)
    start_y()
    for begin, _ in bulk:
        begin()
    slots_y[gy] = mid[...]
    finish_y()
    tile_out[...] = jnp.max(slots_y[...], axis=0)
    for _, end in bulk:
        end()


def wide_gather(nx, ny, blocks, tile):
    count = len(blocks)
    return pl.pallas_call(
        functools.partial(wide_gather_kernel, nx, ny, count),
        out_shape=[jax.ShapeDtypeStruct((ny,) + b.shape, b.dtype) for b in blocks]
        + [jax.ShapeDtypeStruct(tile.shape, tile.dtype)],
        in_specs=[VMEM] * (count + 1),
        out_specs=[VMEM] * (count + 1),
        scratch_shapes=[
            pltpu.VMEM((nx,) + tile.shape, tile.dtype),
            pltpu.VMEM((ny,) + tile.shape, tile.dtype),
            pltpu.VMEM(tile.shape, tile.dtype),
            DMA((count, ny)), DMA((count, ny)),
            DMA((nx,)), DMA((nx,)), DMA((ny,)), DMA((ny,)),
        ],
        compiler_params=pltpu.CompilerParams(collective_id=0, has_side_effects=True),
    )(*blocks, tile)


def chip_scatter_kernel(nx, count, *refs):
    parts, outs = refs[:count], refs[count : 2 * count]
    first = refs[2 * count : 3 * count]
    second = refs[3 * count : 4 * count]
    third = refs[4 * count : 5 * count]
    s1, r1, s2, r2 = refs[5 * count :]
    gx = lax.axis_index("gx")
    y, core = gx // CORES, lax.rem(gx, CORES)
    other = 1 - core
    ys = nx // CORES
    greet(nx, gx, "gx")
    pl.semaphore_wait(pltpu.get_barrier_semaphore(), nx - 1)
    rows = outs[0].shape[0]
    step = 16

    def near(i, k):
        j = lax.rem(y + k, ys)
        return remote(
            parts[i].at[CORES * j + other], first[i].at[k], s1.at[i, k], r1.at[i, k],
            {"gx": CORES * y + other},
        )

    def far(i, k, slot):
        j = lax.rem(y + k, ys)
        return remote(
            second[i].at[k], third[i].at[slot], s2.at[i, k], r2.at[i, k],
            {"gx": CORES * j + core},
        )

    order = list(range(1, ys)) + [0]
    for k in order:
        for i in range(count):
            near(i, k).start()
    for k in order[:-1]:
        j = lax.rem(y + k, ys)
        for i in range(count):
            near(i, k).wait()

            def add(r, i=i, k=k, j=j):
                at = pl.ds(pl.multiple_of(r * step, step), step)
                total = parts[i][CORES * j + core, at, :] + first[i][k, at, :]
                second[i][k, at, :] = total.astype(jnp.bfloat16)

            loop(0, rows // step, add)
            far(i, k, k).start()
    for i in range(count):
        near(i, 0).wait()
    for i in range(count):
        for k in order[:-1]:
            far(i, k, k).wait()

        def close(r, i=i):
            at = pl.ds(pl.multiple_of(r * step, step), step)
            total = parts[i][CORES * y + core, at, :] + first[i][0, at, :]
            for k in order[:-1]:
                total = total + third[i][k, at, :].astype(jnp.float32)
            outs[i][at, :] = total

        loop(0, rows // step, close)


def chip_scatter(nx, parts):
    count, ys = len(parts), nx // CORES
    near = [pltpu.VMEM((ys,) + p.shape[1:], jnp.float32) for p in parts]
    far = [pltpu.VMEM((ys,) + p.shape[1:], jnp.bfloat16) for p in parts]
    return pl.pallas_call(
        functools.partial(chip_scatter_kernel, nx, count),
        out_shape=[jax.ShapeDtypeStruct(p.shape[1:], jnp.float32) for p in parts],
        in_specs=[VMEM] * count,
        out_specs=[VMEM] * count,
        scratch_shapes=near + far * 2
        + [DMA((count, ys)), DMA((count, ys)), DMA((count, ys)), DMA((count, ys))],
        compiler_params=pltpu.CompilerParams(collective_id=1, has_side_effects=True),
    )(*parts)


def chip_gather_kernel(nx, ny, count, *refs):
    blocks, tile = refs[:count], refs[count]
    outs, tile_out = refs[count + 1 : 2 * count + 1], refs[2 * count + 1]
    slots_x, slots_y, mid, sn, rn, sf, rf, sx, rx, sy, ry = refs[2 * count + 2 :]
    gx, gy = lax.axis_index("gx"), lax.axis_index("gy")
    y, core = gx // CORES, lax.rem(gx, CORES)
    other = 1 - core
    ys = nx // CORES
    greet(nx, gx, "gx")
    greet(ny, gy, "gy")
    pl.semaphore_wait(pltpu.get_barrier_semaphore(), nx - 1 + ny - 1)

    start_x, finish_x = exchange(nx, gx, "gx", tile, slots_x, sx, rx)
    start_y, finish_y = exchange(ny, gy, "gy", mid, slots_y, sy, ry)
    start_x()

    def far(i, k, slot):
        j = lax.rem(y + k, ys)
        return remote(
            blocks[i], outs[i].at[slot], sf.at[i, k], rf.at[i, k], {"gx": CORES * j + core}
        )

    def near(i, k, src, slot):
        return remote(
            src, outs[i].at[slot], sn.at[i, k], rn.at[i, k], {"gx": CORES * y + other}
        )

    for k in range(1, ys):
        for i in range(count):
            far(i, k, gx).start()
    for i in range(count):
        near(i, 0, blocks[i], gx).start()
    slots_x[gx] = tile[...]
    for i in range(count):
        outs[i][gx] = blocks[i][...]
    finish_x()
    mid[...] = jnp.max(slots_x[...], axis=0)
    start_y()
    slots_y[gy] = mid[...]
    finish_y()
    tile_out[...] = jnp.max(slots_y[...], axis=0)
    for k in range(1, ys):
        j = lax.rem(y + ys - k, ys)
        mine = CORES * j + core
        for i in range(count):
            far(i, k, mine).wait()
            near(i, k, outs[i].at[mine], mine).start()
    for i in range(count):
        near(i, 0, blocks[i], CORES * y + other).wait()
        for k in range(1, ys):
            j = lax.rem(y + ys - k, ys)
            near(i, k, outs[i].at[CORES * j + core], CORES * j + other).wait()


def chip_gather(nx, ny, blocks, tile):
    count, ys = len(blocks), nx // CORES
    return pl.pallas_call(
        functools.partial(chip_gather_kernel, nx, ny, count),
        out_shape=[jax.ShapeDtypeStruct((nx,) + b.shape, b.dtype) for b in blocks]
        + [jax.ShapeDtypeStruct(tile.shape, tile.dtype)],
        in_specs=[VMEM] * (count + 1),
        out_specs=[VMEM] * (count + 1),
        scratch_shapes=[
            pltpu.VMEM((nx,) + tile.shape, tile.dtype),
            pltpu.VMEM((ny,) + tile.shape, tile.dtype),
            pltpu.VMEM(tile.shape, tile.dtype),
            DMA((count, ys)), DMA((count, ys)), DMA((count, ys)), DMA((count, ys)),
            DMA((nx,)), DMA((nx,)), DMA((ny,)), DMA((ny,)),
        ],
        compiler_params=pltpu.CompilerParams(collective_id=2, has_side_effects=True),
    )(*blocks, tile)


def wide_scatter_kernel(ny, count, *refs):
    parts, outs = refs[:count], refs[count : 2 * count]
    slots = refs[2 * count : 3 * count]
    send, recv = refs[3 * count :]
    gy = lax.axis_index("gy")
    greet(ny, gy, "gy")
    pl.semaphore_wait(pltpu.get_barrier_semaphore(), ny - 1)

    def copy(i, k):
        j = lax.rem(gy + k, ny)
        return remote(
            parts[i].at[j], slots[i].at[k], send.at[i, k], recv.at[i, k], {"gy": j}
        )

    for i in range(count):
        loop(1, ny, lambda k, i=i: copy(i, k).start())
    for i in range(count):
        outs[i][...] = parts[i][gy].astype(jnp.float32)

        def add(k, i=i):
            copy(i, k).wait()
            outs[i][...] += slots[i][k].astype(jnp.float32)

        loop(1, ny, add)


def wide_scatter(ny, parts):
    count = len(parts)
    return pl.pallas_call(
        functools.partial(wide_scatter_kernel, ny, count),
        out_shape=[jax.ShapeDtypeStruct(p.shape[1:], jnp.float32) for p in parts],
        in_specs=[VMEM] * count,
        out_specs=[VMEM] * count,
        scratch_shapes=[pltpu.VMEM(p.shape, p.dtype) for p in parts]
        + [DMA((count, ny)), DMA((count, ny))],
        compiler_params=pltpu.CompilerParams(collective_id=3, has_side_effects=True),
    )(*parts)


def peak_tile(values):
    column = jnp.stack(values + [values[0]] * (8 - len(values)))[:, None]
    return jnp.broadcast_to(column, (8, 128))


def shards(nx, ny, tokens, cotangent, gate_weight, up_weight, down_weight):
    gate_rot = rotate_rows(gate_weight, ROT_BLOCK)
    up_rot = rotate_rows(up_weight, ROT_BLOCK)
    down_rot = rotate_rows(down_weight, HID_BLOCK)
    own_peaks = [
        peak(rotate_cols(tokens, ROT_BLOCK)), peak(gate_rot), peak(up_rot), peak(down_rot)
    ]
    all_tokens, all_cot, peaks = wide_gather(nx, ny, [tokens, cotangent], peak_tile(own_peaks))
    token_peak, gate_peak, up_peak, down_peak = (peaks[i, 0] for i in range(4))
    width = tokens.shape[1]
    all_tokens = all_tokens.reshape(-1, width)
    all_cot = all_cot.reshape(-1, width)
    token_total = all_tokens.shape[0]
    gate_cast = soft_cast(gate_rot, gate_peak)
    up_cast = soft_cast(up_rot, up_peak)
    down_cast = soft_cast(down_rot, down_peak)
    hid_width = gate_weight.shape[1]
    token_cast = soft_cast(rotate_cols(all_tokens, ROT_BLOCK), token_peak)

    def split(matrix, n):
        return matrix.reshape(n, token_total // n, matrix.shape[1])

    gate_sum, up_sum, back_sum = chip_scatter(
        nx,
        [
            split(jnp.dot(token_cast, gate_cast, preferred_element_type=jnp.float32), nx),
            split(jnp.dot(token_cast, up_cast, preferred_element_type=jnp.float32), nx),
            split(contract_cols(all_cot, down_cast), nx),
        ],
    )
    gate_pre = gate_sum * (token_peak * gate_peak / (fp_top * fp_top))
    up_pre = up_sum * (token_peak * up_peak / (fp_top * fp_top))
    sigmoid_gate = jax.nn.sigmoid(gate_pre)
    hidden = (gate_pre * sigmoid_gate * up_pre).astype(jnp.bfloat16)
    own_peak = peak(rotate_cols(hidden, HID_BLOCK))
    hidden_grad = rotate_cols(back_sum * (down_peak / fp_top), HID_BLOCK)
    gate_act = (
        hidden_grad * up_pre * sigmoid_gate * (1.0 + gate_pre * (1.0 - sigmoid_gate))
    ).astype(jnp.bfloat16)
    up_act = (hidden_grad * gate_pre * sigmoid_gate).astype(jnp.bfloat16)
    all_hidden, all_gate_act, all_up_act, tops = chip_gather(
        nx, ny, [hidden, gate_act, up_act], peak_tile([own_peak])
    )
    hidden_peak = tops[0, 0]
    all_hidden = all_hidden.reshape(-1, hid_width)
    all_gate_act = all_gate_act.reshape(-1, hid_width)
    all_up_act = all_up_act.reshape(-1, hid_width)
    hidden_cast = soft_cast(rotate_cols(all_hidden, HID_BLOCK), hidden_peak)
    out_part = jnp.dot(hidden_cast, down_cast, preferred_element_type=jnp.float32)
    input_part = contract_cols(all_gate_act, gate_cast) * (gate_peak / fp_top) + contract_cols(
        all_up_act, up_cast
    ) * (up_peak / fp_top)
    out_sum, input_sum = wide_scatter(
        ny, [split(part.astype(jnp.bfloat16), ny) for part in (out_part, input_part)]
    )
    output = (out_sum * (hidden_peak * down_peak / (fp_top * fp_top))).astype(jnp.bfloat16)
    input_grad = rotate_cols(input_sum, ROT_BLOCK).astype(jnp.bfloat16)
    hidden_turned = rotate_cols(hidden_cast, HID_BLOCK).astype(jnp.bfloat16)
    token_turned = rotate_cols(token_cast, ROT_BLOCK).astype(jnp.bfloat16)
    down_grad = (contract_rows(hidden_turned, all_cot) * (hidden_peak / fp_top)).astype(
        jnp.bfloat16
    )
    gate_grad = (contract_rows(token_turned, all_gate_act) * (token_peak / fp_top)).astype(
        jnp.bfloat16
    )
    up_grad = (contract_rows(token_turned, all_up_act) * (token_peak / fp_top)).astype(jnp.bfloat16)
    return (output, input_grad, gate_grad, up_grad, down_grad)


def solution(mesh):
    in_specs = (P("gy", "gx"), P("gy", "gx"), P("gx", "gy"), P("gx", "gy"), P("gy", "gx"))
    out_specs = (P("gy", "gx"), P("gy", "gx"), P("gx", "gy"), P("gx", "gy"), P("gy", "gx"))
    nx, ny = mesh.shape["gx"], mesh.shape["gy"]
    return jax.shard_map(
        functools.partial(shards, nx, ny),
        mesh=mesh, in_specs=in_specs, out_specs=out_specs, check_vma=False,
    )
```

time: 380 us -> 204 us (0.54)
  blocking collectives: 174 us -> 0 us
  Pallas kernels: 0 us -> 109 us
  waiting for transfers between devices: 84.9 us -> 0 us
  matrix products: 69.2 us -> 48.9 us
  between operations: 24.2 us -> 11.3 us
  local copies, waits for them, and re-layouts: 13 us -> 17.9 us
    pallas_call x0 -> x4, Pallas kernels: none -> 109 us  [the longest x1 32.1 us: wide_gather(): pl.pallas_call(functools.partial(wide_gather_kernel, nx, ny, count), out_...]
    all_gather x5 -> x0, blocking collectives: 92.2 us -> none  [the longest x1 31.6 us: shards(): all_cot = lax.all_gather(cotangent, 'gy', axis=0, tiled=True)]
    reduce_scatter x3 -> x0, waiting for transfers between devices: 84.7 us -> none  [the longest x1 45.3 us: shards(): lax.psum_scatter(contract_cols(all_gate_act, gate_cast) * (gate_peak / fp...]
    pmax x2 -> x0, blocking collectives: 82 us -> none  [the longest x1 42.3 us: shards(): token_peak = lax.pmax(peak(token_rot), ('gx', 'gy'))]
    dot_general x5 -> x3, matrix products: 35.6 us -> 8.88 us  [the longest x1 4.53 us: shards(): jnp.dot(token_cast, up_cast, preferred_element_type=jnp.float32)]
    unnamed x24 -> x41, local copies, waits for them, and re-layouts: 10.9 us -> 3.73 us
    another operation x1 -> x2, local copies, waits for them, and re-layouts: 0.31 us -> 7.29 us  [the longest x1 5.25 us: peak_tile(): column = jnp.stack(values + [values[0]] * (8 - len(values)))[:, None]]
    dot_general x3, matrix products: 3.48 us -> 8.87 us  [contract_rows(): lax.dot_general(left_mat, right_mat, (((0,), (0,)), ((), ())), preferred_...]
  transfers between devices with their start and end apart: 4 -> 0, of which waited for: 4 -> 0; matrix products, arithmetic and copies ran while one was open for 14% -> 0% of each run, Pallas kernels for 0% -> 0%
where the time goes in v1:
time: 204 us; the launch traced here: 203 us
  Pallas kernels  109 us (53%)
  matrix products  48.9 us (24%)
  local copies, waits for them, and re-layouts  17.9 us (9%)
  other arithmetic  16 us (8%)
  between operations  11.3 us (6%)
    pallas_call x1, Pallas kernels, wide_gather(): pl.pallas_call(functools.partial(wide_gather_kernel, nx, ny, count), out_...  32.1 us
    pallas_call x1, Pallas kernels, chip_gather(): pl.pallas_call(functools.partial(chip_gather_kernel, nx, ny, count), out_...  27.4 us
    pallas_call x1, Pallas kernels, wide_scatter(): pl.pallas_call(functools.partial(wide_scatter_kernel, ny, count), out_sha...  26.2 us
    pallas_call x1, Pallas kernels, chip_scatter(): pl.pallas_call(functools.partial(chip_scatter_kernel, nx, count), out_sha...  23.6 us
    dot_general x3, matrix products, rotate_rows(): jnp.einsum('kl,bkc->blc', table.astype(jnp.bfloat16), blocks, preferred_e...  16.3 us
    another operation x3, other arithmetic  12.3 us
    dot_general x3, matrix products, contract_rows(): lax.dot_general(left_mat, right_mat, (((0,), (0,)), ((), ())), preferred_...  8.87 us
    dot_general x3, matrix products, contract_cols(): lax.dot_general(left_mat, right_mat, (((1,), (1,)), ((), ())), preferred_...  8.02 us

profile of v1, /device:TPU:0, one launch (start us, length us, event | category | flops | bytes accessed | tf_op | source)
XLA Modules:
  0.0 203.4 jit_solution(9674418614757923433)
XLA Ops:
  0.6 1.7 fusion.24
  2.3 6.9 %abs_reduce_fusion.2 = (f32[]{:T(128)}, f32[128,8,1792]{2,0,1:T(8,128)}) fusion(bf16[8,128,1792]{2,1,0:T(8,128)(2,1)} %bitcast.135), kind=kOutput, calls=%fused_computation.8 | convolution fusion | flops 475856896 | bytes 11010052 | tf_op jit(solution)/shard_map/kl,bkc->blc/dot_general | solution.py:49
  9.2 4.8 %abs_reduce_fusion.1 = (f32[]{:T(128)}, f32[128,8,1792]{2,0,1:T(8,128)}) fusion(bf16[8,128,1792]{2,1,0:T(8,128)(2,1)S(1)} %bitcast.136), kind=kOutput, calls=%fused_computation.7 | convolution fusion | flops 475856896 | bytes 11010052 | tf_op jit(solution)/shard_map/kl,bkc->blc/dot_general | solution.py:49
  13.9 4.7 %abs_reduce_fusion = (f32[]{:T(128)}, f32[64,28,1024]{2,0,1:T(8,128)}) fusion(bf16[28,64,1024]{2,1,0:T(8,128)(2,1)S(1)} %bitcast.137), kind=kOutput, calls=%fused_computation.6 | convolution fusion | flops 240521216 | bytes 11010052 | tf_op jit(solution)/shard_map/kl,bkc->blc/dot_general | solution.py:49
  18.6 5.2 %stack.14 = f32[8]{0:T(128)S(1)} concatenate(f32[1]{0:T(128)} %bitcast.1, f32[1]{0:T(128)} %bitcast.4, f32[1]{0:T(128)} %bitcast.6, f32[1]{0:T(128)} %bitcast.9, f32[1]{0:T(128)} %bitcast.1, f32[1]{0:T(128)} %bitcast.1, f32[1]{0:T(128)} %bitcast.1, f32[1]{0:T(128)} %bitcast.1), dimensions={0} | concatenate | bytes 64 | tf_op jit(solution)/shard_map/stack | solution.py:353
  24.5 32.1 %shard_map.92 = (bf16[8,32,1024]{2,1,0:T(8,128)(2,1)}, bf16[8,32,1024]{2,1,0:T(8,128)(2,1)}, f32[8,128]{1,0:T(8,128)}) custom-call(bf16[32,1024]{1,0:T(8,128)(2,1)} %refs_0_.1, bf16[32,1024]{1,0:T(8,128)(2,1)} %refs_1_.1, f32[8,128]{1,0:T(8,128)} %broadcast_in_dim.4.refs_2_), custom_call_target="tpu_custom_call" | custom-call | tf_op jit(solution)/shard_map/pallas_call | solution.py:147
  56.7 1.3 copy.49
  58.0 1.3 fusion.136
  67.1 6.3 %multiply_convert_fusion.3 = bf16[64,28,1024]{2,0,1:T(8,128)(2,1)} fusion(f32[64,28,1024]{2,0,1:T(8,128)} %get-tuple-element.41, f32[]{:T(128)} %bitcast.21), kind=kLoop, calls=%fused_computation.3 | loop fusion | flops 7340032 | bytes 11010052 | tf_op jit(solution)/shard_map/convert
  73.4 3.0 %multiply_convert_fusion.4 = bf16[128,8,1792]{2,0,1:T(8,128)(2,1)} fusion(f32[128,8,1792]{2,0,1:T(8,128)S(1)} %bitcast.130, f32[]{:T(128)} %bitcast.16), kind=kLoop, calls=%fused_computation.4 | loop fusion | flops 7340032 | bytes 11010052 | tf_op jit(solution)/shard_map/convert.1
  76.4 3.0 %multiply_convert_fusion.5 = bf16[128,8,1792]{2,0,1:T(8,128)(2,1)} fusion(f32[128,8,1792]{2,0,1:T(8,128)S(1)} %bitcast.128, f32[]{:T(128)} %bitcast.12), kind=kLoop, calls=%fused_computation.5 | loop fusion | flops 7340032 | bytes 11010052 | tf_op jit(solution)/shard_map/convert.2
  81.0 4.5 %fusion.138.refs_1_ = f32[4,64,1792]{2,1,0:T(8,128)} fusion(bf16[4,64,1024]{2,1,0:T(8,128)(2,1)S(1)} %convert_element_type.141, bf16[1024,1792,1]{1,0,2:T(8,128)(2,1)} %bitcast.131), kind=kOutput, calls=%fused_computation.153 | convolution fusion | flops 939524096 | bytes 6029312 | tf_op jit(solution)/shard_map/dot_general | solution.py:383
  85.5 2.4 %fusion.137.refs_0_ = f32[4,64,1792]{2,1,0:T(8,128)} fusion(bf16[4,64,1024]{2,1,0:T(8,128)(2,1)S(1)} %convert_element_type.141, bf16[1024,1792,1]{1,0,2:T(8,128)(2,1)S(1)} %bitcast.133), kind=kOutput, calls=%fused_computation.152 | convolution fusion | flops 939524096 | bytes 6029312 | tf_op jit(solution)/shard_map/dot_general | solution.py:382
  87.9 2.5 %fusion.139.refs_2_ = f32[4,64,1792]{2,1,0:T(8,128)} fusion(bf16[4,64,1024]{2,1,0:T(8,128)(2,1)S(1)} %bitcast.154, bf16[1792,1024,1]{1,0,2:T(8,128)(2,1)S(1)} %bitcast.138), kind=kOutput, calls=%fused_computation.154 | convolution fusion | flops 939524096 | bytes 6029312 | tf_op jit(solution)/shard_map/dot_general | solution.py:70
  90.4 23.6 %shard_map.93 = (f32[64,1792]{1,0:T(8,128)}, f32[64,1792]{1,0:T(8,128)}, f32[64,1792]{1,0:T(8,128)}) custom-call(f32[4,64,1792]{2,1,0:T(8,128)} %fusion.137.refs_0_, f32[4,64,1792]{2,1,0:T(8,128)} %fusion.138.refs_1_, f32[4,64,1792]{2,1,0:T(8,128)} %fusion.139.refs_2_), custom_call_target="tpu_custom_call" | custom-call | tf_op jit(solution)/shard_map/pallas_call | solution.py:229
  114.0 1.1 broadcast_multiply_fusion
  115.5 1.5 convolution_multiply_fusion.4
  117.9 1.0 multiply_convert_fusion.8
  119.5 1.0 fusion.23
  120.5 1.1 broadcast_in_dim.5.refs_3_
  121.6 27.4 %shard_map.94 = (bf16[4,64,1792]{2,1,0:T(8,128)(2,1)}, bf16[4,64,1792]{2,1,0:T(8,128)(2,1)}, bf16[4,64,1792]{2,1,0:T(8,128)(2,1)}, f32[8,128]{1,0:T(8,128)}) custom-call(bf16[64,1792]{1,0:T(8,128)(2,1)} %copy-done.6, bf16[64,1792]{1,0:T(8,128)(2,1)} %get-tuple-element.30.refs_1_, bf16[64,1792]{1,0:T(8,128)(2,1)} %get-tuple-element.29.refs_2_, ...), custom_call_target="tpu_custom_call" | custom-call | tf_op jit(solution)/shard_map/pallas_call | solution.py:296
  149.0 3.6 %convolution_multiply_fusion = f32[256,1024]{1,0:T(8,128)S(1)} fusion(bf16[256,1792]{1,0:T(8,128)(2,1)} %bitcast.150, bf16[1024,1792]{1,0:T(8,128)(2,1)} %bitcast.132, f32[]{:T(128)} %bitcast.38), kind=kOutput, calls=%fused_computation.16 | convolution fusion | flops 939786240 | bytes 5636100 | tf_op jit(solution)/shard_map/dot_general | solution.py:70
  152.7 1.9 fusion.15
  154.6 1.2 slice.19
  158.4 2.0 %reshape.140 = bf16[256,28,64]{2,1,0:T(8,128)(2,1)S(1)} reshape(bf16[4,64,1792]{2,1,0:T(8,128)(2,1)S(1)} %copy-done.7) | data formatting | bytes 1835008 | tf_op jit(solution)/shard_map/reshape;reshape | solution.py:35
  160.5 1.2 multiply_convert_fusion.7
  162.5 1.9 fusion.17
  164.9 26.2 %shard_map.95 = (f32[32,1024]{1,0:T(8,128)}, f32[32,1024]{1,0:T(8,128)}) custom-call(bf16[8,32,1024]{2,1,0:T(8,128)(2,1)} %bitcast.144, bf16[8,32,1024]{2,1,0:T(8,128)(2,1)} %bitcast.143), custom_call_target="tpu_custom_call" | custom-call | tf_op jit(solution)/shard_map/pallas_call | solution.py:341
  191.0 1.5 multiply_convert_fusion.11
  194.5 3.0 %multiply_convert_fusion = bf16[1792,1024]{1,0:T(8,128)(2,1)} fusion(bf16[256,1792]{0,1:T(8,128)(2,1)S(1)} %bitcast.139, bf16[256,1024]{1,0:T(8,128)(2,1)S(1)} %bitcast.155, f32[]{:T(128)} %bitcast.46), kind=kOutput, calls=%fused_computation | convolution fusion | flops 943194112 | bytes 5111812 | tf_op jit(solution)/shard_map/dot_general | solution.py:64
  197.5 3.0 %multiply_convert_fusion.2 = bf16[1024,1792]{1,0:T(8,128)(2,1)} fusion(bf16[256,1024]{0,1:T(8,128)(2,1)S(1)} %bitcast.140, bf16[256,1792]{1,0:T(8,128)(2,1)S(1)} %bitcast.153, f32[]{:T(128)} %bitcast.43), kind=kOutput, calls=%fused_computation.2 | convolution fusion | flops 943194112 | bytes 5111812 | tf_op jit(solution)/shard_map/dot_general | solution.py:64
  200.4 3.0 %multiply_convert_fusion.1 = bf16[1024,1792]{1,0:T(8,128)(2,1)} fusion(bf16[256,1024]{0,1:T(8,128)(2,1)S(1)} %bitcast.141, bf16[256,1792]{1,0:T(8,128)(2,1)S(1)} %bitcast.151, f32[]{:T(128)} %bitcast.43), kind=kOutput, calls=%fused_computation.1 | convolution fusion | flops 943194112 | bytes 5111812 | tf_op jit(solution)/shard_map/dot_general | solution.py:64
  (54 shorter events, 7.2 us)
Async XLA Ops:
  2.3 6.9 %copy-start.2 = (bf16[1024,1792]{1,0:T(8,128)(2,1)S(1)}, bf16[1024,1792]{1,0:T(8,128)(2,1)}, u32[]{:S(2)}) copy-start(bf16[1024,1792]{1,0:T(8,128)(2,1)} %param.8) | copy-start | bytes 11010052
  9.2 4.8 %copy-start.3 = (bf16[1792,1024]{1,0:T(8,128)(2,1)S(1)}, bf16[1792,1024]{1,0:T(8,128)(2,1)}, u32[]{:S(2)}) copy-start(bf16[1792,1024]{1,0:T(8,128)(2,1)} %param.9) | copy-start | bytes 11010052
  13.9 59.5 %slice-start.2 = ((s8[7340032]{0:T(1024)(128)(4,1)}), s8[3145728]{0:T(1024)(128)(4,1)S(1)}, s32[]{:S(2)}) async-start(s8[7340032]{0:T(1024)(128)(4,1)} %bitcast.129), calls=%async_computation.2 | async-start | bytes 6291456
  56.7 16.7 %slice-start.3 = ((s8[7340032]{0:T(1024)(128)(4,1)}), s8[4194304]{0:T(1024)(128)(4,1)S(1)}, s32[]{:S(2)}) async-start(s8[7340032]{0:T(1024)(128)(4,1)} %bitcast.129), calls=%async_computation.3 | async-start | bytes 8388608
  67.1 9.3 %slice-start = ((s8[7340032]{0:T(1024)(128)(4,1)}), s8[4194304]{0:T(1024)(128)(4,1)S(1)}, s32[]{:S(2)}) async-start(s8[7340032]{0:T(1024)(128)(4,1)} %bitcast.127), calls=%async_computation | async-start | bytes 8388608
  73.4 3.0 %slice-start.1 = ((s8[7340032]{0:T(1024)(128)(4,1)}), s8[3145728]{0:T(1024)(128)(4,1)S(1)}, s32[]{:S(2)}) async-start(s8[7340032]{0:T(1024)(128)(4,1)} %bitcast.127), calls=%async_computation.1 | async-start | bytes 6291456
  80.9 4.5 %copy-start = (bf16[128,8,1792]{2,0,1:T(8,128)(2,1)S(1)}, bf16[128,8,1792]{2,0,1:T(8,128)(2,1)}, u32[]{:S(2)}) copy-start(bf16[128,8,1792]{2,0,1:T(8,128)(2,1)} %multiply_convert_fusion.5) | copy-start | bytes 11010052
  85.5 2.4 %copy-start.4 = (bf16[64,28,1024]{2,0,1:T(8,128)(2,1)S(1)}, bf16[64,28,1024]{2,0,1:T(8,128)(2,1)}, u32[]{:S(2)}) copy-start(bf16[64,28,1024]{2,0,1:T(8,128)(2,1)} %multiply_convert_fusion.3) | copy-start | bytes 11010052
  85.5 2.4 %copy-start.13 = (bf16[8,32,1024]{2,1,0:T(8,128)(2,1)S(1)}, bf16[8,32,1024]{2,1,0:T(8,128)(2,1)}, u32[]{:S(2)}) copy-start(bf16[8,32,1024]{2,1,0:T(8,128)(2,1)} %get-tuple-element.19) | copy-start | bytes 1572868
  113.9 4.0 %copy-start.8 = (f32[64,1792]{1,0:T(8,128)S(1)}, f32[64,1792]{1,0:T(8,128)}, u32[]{:S(2)}) copy-start(f32[64,1792]{1,0:T(8,128)} %get-tuple-element.20) | copy-start | bytes 1376260
  113.9 4.0 %copy-start.9 = (f32[64,1792]{1,0:T(8,128)S(1)}, f32[64,1792]{1,0:T(8,128)}, u32[]{:S(2)}) copy-start(f32[64,1792]{1,0:T(8,128)} %get-tuple-element.21) | copy-start | bytes 1376260
  119.0 2.6 %copy-start.6 = (bf16[64,1792]{1,0:T(8,128)(2,1)}, bf16[64,1792]{1,0:T(8,128)(2,1)S(1)}, u32[]{:S(2)}) copy-start(bf16[64,1792]{1,0:T(8,128)(2,1)S(1)} %get-tuple-element.31.refs_0_) | copy-start | bytes 688132
  149.0 3.7 %copy-start.1 = (bf16[128,8,1792]{2,0,1:T(8,128)(2,1)S(1)}, bf16[128,8,1792]{2,0,1:T(8,128)(2,1)}, u32[]{:S(2)}) copy-start(bf16[128,8,1792]{2,0,1:T(8,128)(2,1)} %multiply_convert_fusion.5) | copy-start | bytes 11010052
  149.0 3.7 %copy-start.11 = (bf16[4,64,1792]{2,1,0:T(8,128)(2,1)S(1)}, bf16[4,64,1792]{2,1,0:T(8,128)(2,1)}, u32[]{:S(2)}) copy-start(bf16[4,64,1792]{2,1,0:T(8,128)(2,1)} %get-tuple-element.25) | copy-start | bytes 2752516
  152.7 5.8 %copy-start.7 = (bf16[4,64,1792]{2,1,0:T(8,128)(2,1)S(1)}, bf16[4,64,1792]{2,1,0:T(8,128)(2,1)}, u32[]{:S(2)}) copy-start(bf16[4,64,1792]{2,1,0:T(8,128)(2,1)} %get-tuple-element.23) | copy-start | bytes 2752516
  160.5 2.0 %copy-start.5 = (bf16[64,28,1024]{2,0,1:T(8,128)(2,1)S(1)}, bf16[64,28,1024]{2,0,1:T(8,128)(2,1)}, u32[]{:S(2)}) copy-start(bf16[64,28,1024]{2,0,1:T(8,128)(2,1)} %multiply_convert_fusion.3) | copy-start | bytes 11010052
  164.5 30.0 %copy-start.14 = (bf16[8,32,1024]{2,1,0:T(8,128)(2,1)S(1)}, bf16[8,32,1024]{2,1,0:T(8,128)(2,1)}, u32[]{:S(2)}) copy-start(bf16[8,32,1024]{2,1,0:T(8,128)(2,1)} %get-tuple-element.19) | copy-start | bytes 1572868
  194.5 3.0 %copy-start.12 = (bf16[4,64,1792]{2,1,0:T(8,128)(2,1)S(1)}, bf16[4,64,1792]{2,1,0:T(8,128)(2,1)}, u32[]{:S(2)}) copy-start(bf16[4,64,1792]{2,1,0:T(8,128)(2,1)} %get-tuple-element.25) | copy-start | bytes 2752516
  197.5 3.0 %copy-start.10 = (bf16[4,64,1792]{2,1,0:T(8,128)(2,1)S(1)}, bf16[4,64,1792]{2,1,0:T(8,128)(2,1)}, u32[]{:S(2)}) copy-start(bf16[4,64,1792]{2,1,0:T(8,128)(2,1)} %get-tuple-element.26) | copy-start | bytes 2752516

commit v2 on v1

v2 whole, which is shorter than its diff:
```python
import functools

import jax
import jax.numpy as jnp
from jax import lax
from jax.experimental import pallas as pl
from jax.experimental.pallas import tpu as pltpu
from jax.sharding import PartitionSpec as P

ROT_BLOCK = 128
HID_BLOCK = 64
CORES = 2

fp_top = 448.0
tiny = 1e-06

MESH = pl.DeviceIdType.MESH
VMEM = pl.BlockSpec(memory_space=pltpu.VMEM)
DMA = pltpu.SemaphoreType.DMA


def hadamard_table(block_size):
    row_ids = jnp.arange(block_size, dtype=jnp.int32)[:, None]
    col_ids = jnp.arange(block_size, dtype=jnp.int32)[None, :]
    shared = row_ids & col_ids
    parity = jnp.zeros((block_size, block_size), jnp.int32)
    for bit_pos in range(max(block_size.bit_length() - 1, 1)):
        parity = parity + (shared >> bit_pos & 1)
    return (1 - 2 * (parity % 2)).astype(jnp.float32)


def rotate_cols(matrix, block_size):
    row_total, col_total = matrix.shape
    table = hadamard_table(block_size)
    blocks = matrix.reshape(row_total, col_total // block_size, block_size)
    if matrix.dtype == jnp.bfloat16:
        turned = jnp.einsum(
            "rbk,kl->rbl", blocks, table.astype(jnp.bfloat16), preferred_element_type=jnp.float32
        )
    else:
        turned = jnp.einsum("rbk,kl->rbl", blocks, table, precision=lax.Precision.HIGHEST)
    return turned.reshape(row_total, col_total) * block_size ** (-0.5)


def rotate_rows(matrix, block_size):
    row_total, col_total = matrix.shape
    table = hadamard_table(block_size)
    blocks = matrix.reshape(row_total // block_size, block_size, col_total)
    turned = jnp.einsum(
        "kl,bkc->blc", table.astype(jnp.bfloat16), blocks, preferred_element_type=jnp.float32
    )
    return turned.reshape(row_total, col_total) * block_size ** (-0.5)


def soft_cast(values, top):
    return (fp_top * jnp.tanh(values / top)).astype(jnp.bfloat16)


def peak(values):
    return jnp.max(jnp.abs(values))


def contract_rows(left_mat, right_mat):
    return lax.dot_general(
        left_mat, right_mat, (((0,), (0,)), ((), ())), preferred_element_type=jnp.float32
    )


def contract_cols(left_mat, right_mat):
    return lax.dot_general(
        left_mat, right_mat, (((1,), (1,)), ((), ())), preferred_element_type=jnp.float32
    )


def remote(src, dst, send, recv, target):
    return pltpu.make_async_remote_copy(
        src_ref=src, dst_ref=dst, send_sem=send, recv_sem=recv,
        device_id=target, device_id_type=MESH,
    )


def loop(low, high, body):
    def step(i, carry):
        body(i)
        return carry
    lax.fori_loop(low, high, step, 0)


def greet(n, me, axis):
    barrier = pltpu.get_barrier_semaphore()

    def hello(k):
        pl.semaphore_signal(
            barrier, inc=1, device_id={axis: lax.rem(me + k, n)}, device_id_type=MESH
        )

    loop(1, n, hello)


def exchange(n, me, axis, src, slots, send, recv):
    def copy(k, slot):
        return remote(
            src, slots.at[slot], send.at[k], recv.at[k], {axis: lax.rem(me + k, n)}
        )

    def start(k):
        copy(k, me).start()

    def finish(k):
        copy(k, lax.rem(me + n - k, n)).wait()

    return (lambda: loop(1, n, start)), (lambda: loop(1, n, finish))


def scatter_kernel(axis, n, inner, count, *refs):
    parts, outs = refs[:count], refs[count : 2 * count]
    first = refs[2 * count : 3 * count]
    second = refs[3 * count : 4 * count]
    third = refs[4 * count : 5 * count]
    s1, r1, s2, r2 = refs[5 * count :]
    me = lax.axis_index(axis)
    hi, lo = me // inner, lax.rem(me, inner)
    outer = n // inner
    greet(n, me, axis)
    pl.semaphore_wait(pltpu.get_barrier_semaphore(), n - 1)
    rows = outs[0].shape[0]
    step = 16

    def near(i, k, o):
        j, to = lax.rem(hi + k, outer), lax.rem(lo + o, inner)
        return remote(
            parts[i].at[inner * j + to], first[i].at[k * inner + o], s1.at[i, k, o],
            r1.at[i, k, o], {axis: inner * hi + to},
        )

    def far(i, k):
        j = lax.rem(hi + k, outer)
        return remote(
            second[i].at[k], third[i].at[k], s2.at[i, k], r2.at[i, k], {axis: inner * j + lo}
        )

    def inner_sum(i, k, at):
        total = parts[i][inner * lax.rem(hi + k, outer) + lo, at, :].astype(jnp.float32)
        for o in range(1, inner):
            total = total + first[i][k * inner + o, at, :].astype(jnp.float32)
        return total

    order = list(range(1, outer)) + [0]
    for k in order:
        for i in range(count):
            for o in range(1, inner):
                near(i, k, o).start()
    for k in order[:-1]:
        for i in range(count):
            for o in range(1, inner):
                near(i, k, o).wait()

            def add(r, i=i, k=k):
                at = pl.ds(pl.multiple_of(r * step, step), step)
                second[i][k, at, :] = inner_sum(i, k, at).astype(jnp.bfloat16)

            loop(0, rows // step, add)
            far(i, k).start()
    for i in range(count):
        for o in range(1, inner):
            near(i, 0, o).wait()
    for i in range(count):
        for k in order[:-1]:
            far(i, k).wait()

        def close(r, i=i):
            at = pl.ds(pl.multiple_of(r * step, step), step)
            total = inner_sum(i, 0, at)
            for k in order[:-1]:
                total = total + third[i][k, at, :].astype(jnp.float32)
            outs[i][at, :] = total

        loop(0, rows // step, close)


def scatter(axis, n, inner, parts, number):
    count, outer = len(parts), n // inner
    near = [pltpu.VMEM((n,) + p.shape[1:], p.dtype) for p in parts]
    far = [pltpu.VMEM((outer,) + p.shape[1:], jnp.bfloat16) for p in parts]
    return pl.pallas_call(
        functools.partial(scatter_kernel, axis, n, inner, count),
        out_shape=[jax.ShapeDtypeStruct(p.shape[1:], jnp.float32) for p in parts],
        in_specs=[VMEM] * count,
        out_specs=[VMEM] * count,
        scratch_shapes=near + far * 2
        + [DMA((count, outer, inner))] * 2 + [DMA((count, outer))] * 2,
        compiler_params=pltpu.CompilerParams(collective_id=number, has_side_effects=True),
    )(*parts)


def gather_kernel(axis, n, inner, nx, ny, count, *refs):
    blocks, tile = refs[:count], refs[count]
    outs, tile_out = refs[count + 1 : 2 * count + 1], refs[2 * count + 1]
    slots_x, slots_y, mid, sn, rn, sf, rf, sx, rx, sy, ry = refs[2 * count + 2 :]
    gx, gy = lax.axis_index("gx"), lax.axis_index("gy")
    me = lax.axis_index(axis)
    hi, lo = me // inner, lax.rem(me, inner)
    outer = n // inner
    greet(nx, gx, "gx")
    greet(ny, gy, "gy")
    pl.semaphore_wait(pltpu.get_barrier_semaphore(), nx - 1 + ny - 1)

    start_x, finish_x = exchange(nx, gx, "gx", tile, slots_x, sx, rx)
    start_y, finish_y = exchange(ny, gy, "gy", mid, slots_y, sy, ry)
    start_x()

    def far(i, k, slot):
        j = lax.rem(hi + k, outer)
        return remote(
            blocks[i], outs[i].at[slot], sf.at[i, k], rf.at[i, k], {axis: inner * j + lo}
        )

    def near(i, k, o, src, slot):
        return remote(
            src, outs[i].at[slot], sn.at[i, k, o], rn.at[i, k, o],
            {axis: inner * hi + lax.rem(lo + o, inner)},
        )

    for k in range(1, outer):
        for i in range(count):
            far(i, k, me).start()
    for i in range(count):
        for o in range(1, inner):
            near(i, 0, o, blocks[i], me).start()
    slots_x[gx] = tile[...]
    for i in range(count):
        outs[i][me] = blocks[i][...]
    finish_x()
    mid[...] = jnp.max(slots_x[...], axis=0)
    start_y()
    slots_y[gy] = mid[...]
    for k in range(1, outer):
        mine = inner * lax.rem(hi + outer - k, outer) + lo
        for i in range(count):
            far(i, k, mine).wait()
            for o in range(1, inner):
                near(i, k, o, outs[i].at[mine], mine).start()
    finish_y()
    top = jnp.max(slots_y[...], axis=0)
    tile_out[0] = top
    tile_out[1] = top + tiny
    tile_out[2] = top / fp_top
    tile_out[3] = top * top[0:1, :] / (fp_top * fp_top)
    for i in range(count):
        for o in range(1, inner):
            side = lax.rem(lo + inner - o, inner)
            near(i, 0, o, blocks[i], inner * hi + side).wait()
            for k in range(1, outer):
                row = inner * lax.rem(hi + outer - k, outer)
                near(i, k, o, outs[i].at[row + lo], row + side).wait()


def gather(axis, n, inner, nx, ny, blocks, tile, number):
    count, outer = len(blocks), n // inner
    return pl.pallas_call(
        functools.partial(gather_kernel, axis, n, inner, nx, ny, count),
        out_shape=[jax.ShapeDtypeStruct((n,) + b.shape, b.dtype) for b in blocks]
        + [jax.ShapeDtypeStruct((4,) + tile.shape, tile.dtype)],
        in_specs=[VMEM] * (count + 1),
        out_specs=[VMEM] * (count + 1),
        scratch_shapes=[
            pltpu.VMEM((nx,) + tile.shape, tile.dtype),
            pltpu.VMEM((ny,) + tile.shape, tile.dtype),
            pltpu.VMEM(tile.shape, tile.dtype),
        ]
        + [DMA((count, outer, inner))] * 2 + [DMA((count, outer))] * 2
        + [DMA((nx,))] * 2 + [DMA((ny,))] * 2,
        compiler_params=pltpu.CompilerParams(collective_id=number, has_side_effects=True),
    )(*blocks, tile)


def peak_tile(values):
    rows = lax.broadcasted_iota(jnp.int32, (8, 128), 0)
    tile = jnp.full((8, 128), values[0])
    for i, value in enumerate(values[1:], 1):
        tile = jnp.where(rows == i, value, tile)
    return tile


def shards(nx, ny, tokens, cotangent, gate_weight, up_weight, down_weight):
    lanes = 1 << ((ny.bit_length() - 2) // 2)
    gate_rot = rotate_rows(gate_weight, ROT_BLOCK)
    up_rot = rotate_rows(up_weight, ROT_BLOCK)
    down_rot = rotate_rows(down_weight, HID_BLOCK)
    own_peaks = [
        peak(rotate_cols(tokens, ROT_BLOCK)), peak(gate_rot), peak(up_rot), peak(down_rot)
    ]
    all_tokens, all_cot, peaks = gather(
        "gy", ny, lanes, nx, ny, [tokens, cotangent], peak_tile(own_peaks), 0
    )
    down_peak = peaks[0, 3, 0]
    token_top, gate_top, up_top, down_top = (peaks[1, i, 0] for i in range(4))
    token_unit, gate_unit, up_unit, down_unit = (peaks[2, i, 0] for i in range(4))
    width = tokens.shape[1]
    all_tokens = all_tokens.reshape(-1, width)
    all_cot = all_cot.reshape(-1, width)
    token_total = all_tokens.shape[0]
    gate_cast = soft_cast(gate_rot, gate_top)
    up_cast = soft_cast(up_rot, up_top)
    down_cast = soft_cast(down_rot, down_top)
    hid_width = gate_weight.shape[1]
    token_cast = soft_cast(rotate_cols(all_tokens, ROT_BLOCK), token_top)

    def split(matrix, n):
        return matrix.reshape(n, token_total // n, matrix.shape[1])

    gate_sum, up_sum, back_sum = scatter(
        "gx", nx, CORES,
        [
            split(jnp.dot(token_cast, gate_cast, preferred_element_type=jnp.float32), nx),
            split(jnp.dot(token_cast, up_cast, preferred_element_type=jnp.float32), nx),
            split(contract_cols(all_cot, down_cast), nx),
        ],
        1,
    )
    gate_pre = gate_sum * peaks[3, 1, 0]
    up_pre = up_sum * peaks[3, 2, 0]
    sigmoid_gate = jax.nn.sigmoid(gate_pre)
    hidden = (gate_pre * sigmoid_gate * up_pre).astype(jnp.bfloat16)
    own_peak = peak(rotate_cols(hidden, HID_BLOCK))
    hidden_grad = rotate_cols(back_sum * down_unit, HID_BLOCK)
    gate_act = (
        hidden_grad * up_pre * sigmoid_gate * (1.0 + gate_pre * (1.0 - sigmoid_gate))
    ).astype(jnp.bfloat16)
    up_act = (hidden_grad * gate_pre * sigmoid_gate).astype(jnp.bfloat16)
    all_hidden, all_gate_act, all_up_act, tops = gather(
        "gx", nx, CORES, nx, ny, [hidden, gate_act, up_act], peak_tile([own_peak, down_peak]), 2
    )
    hidden_top, hidden_unit = tops[1, 0, 0], tops[2, 0, 0]
    all_hidden = all_hidden.reshape(-1, hid_width)
    all_gate_act = all_gate_act.reshape(-1, hid_width)
    all_up_act = all_up_act.reshape(-1, hid_width)
    hidden_cast = soft_cast(rotate_cols(all_hidden, HID_BLOCK), hidden_top)
    out_part = jnp.dot(hidden_cast, down_cast, preferred_element_type=jnp.float32)
    input_part = contract_cols(all_gate_act, gate_cast) * gate_unit + contract_cols(
        all_up_act, up_cast
    ) * up_unit
    out_sum, input_sum = scatter(
        "gy", ny, lanes,
        [split(part.astype(jnp.bfloat16), ny) for part in (out_part, input_part)],
        3,
    )
    output = (out_sum * tops[3, 1, 0]).astype(jnp.bfloat16)
    input_grad = rotate_cols(input_sum, ROT_BLOCK).astype(jnp.bfloat16)
    hidden_turned = rotate_cols(hidden_cast, HID_BLOCK).astype(jnp.bfloat16)
    token_turned = rotate_cols(token_cast, ROT_BLOCK).astype(jnp.bfloat16)
    down_grad = (contract_rows(hidden_turned, all_cot) * hidden_unit).astype(
        jnp.bfloat16
    )
    gate_grad = (contract_rows(token_turned, all_gate_act) * token_unit).astype(
        jnp.bfloat16
    )
    up_grad = (contract_rows(token_turned, all_up_act) * token_unit).astype(jnp.bfloat16)
    return (output, input_grad, gate_grad, up_grad, down_grad)


def solution(mesh):
    in_specs = (P("gy", "gx"), P("gy", "gx"), P("gx", "gy"), P("gx", "gy"), P("gy", "gx"))
    out_specs = (P("gy", "gx"), P("gy", "gx"), P("gx", "gy"), P("gx", "gy"), P("gy", "gx"))
    nx, ny = mesh.shape["gx"], mesh.shape["gy"]
    return jax.shard_map(
        functools.partial(shards, nx, ny),
        mesh=mesh, in_specs=in_specs, out_specs=out_specs, check_vma=False,
    )
```

time: 204 us -> 187 us (0.917)
  Pallas kernels: 109 us -> 95.1 us
  between operations: 11.3 us -> 0.94 us
  other arithmetic: 16 us -> 25.1 us
  local copies, waits for them, and re-layouts: 17.9 us -> 11.4 us
  matrix products: 48.9 us -> 54.2 us
    pallas_call x4, Pallas kernels: 109 us -> 95.1 us  [the longest x2 50.8 us: gather(): pl.pallas_call(functools.partial(gather_kernel, axis, n, inner, nx, ny, c...]
    another operation x1 -> x0, local copies, waits for them, and re-layouts: 5.25 us -> none  [peak_tile(): column = jnp.stack(values + [values[0]] * (8 - len(values)))[:, None]]
    select_n x0 -> x3, other arithmetic: none -> 4.59 us  [peak_tile(): tile = jnp.where(rows == i, value, tile)]
where the time goes in v2:
time: 187 us
  Pallas kernels  95.1 us (51%)
  matrix products  54.2 us (29%)
  other arithmetic  25.1 us (13%)
  local copies, waits for them, and re-layouts  11.4 us (6%)
    pallas_call x2, Pallas kernels, gather(): pl.pallas_call(functools.partial(gather_kernel, axis, n, inner, nx, ny, c...  50.8 us
    pallas_call x2, Pallas kernels, scatter(): pl.pallas_call(functools.partial(scatter_kernel, axis, n, inner, count),...  44.3 us
    dot_general x3, matrix products, rotate_rows(): jnp.einsum('kl,bkc->blc', table.astype(jnp.bfloat16), blocks, preferred_e...  16.3 us
    another operation x3, other arithmetic  14.2 us
    dot_general x3, matrix products, contract_rows(): lax.dot_general(left_mat, right_mat, (((0,), (0,)), ((), ())), preferred_...  10.8 us
    dot_general x3, matrix products, contract_cols(): lax.dot_general(left_mat, right_mat, (((1,), (1,)), ((), ())), preferred_...  9.78 us
    dot_general x6, matrix products, rotate_cols(): jnp.einsum('rbk,kl->rbl', blocks, table.astype(jnp.bfloat16), preferred_e...  6.61 us
    select_n x3, other arithmetic, peak_tile(): tile = jnp.where(rows == i, value, tile)  4.59 us

profile of v2, /device:TPU:0, one launch (start us, length us, event | category | flops | bytes accessed | tf_op | source)
XLA Modules:
  0.0 186.8 jit_solution(14934206638692672424)
XLA Ops:
  0.6 1.7 fusion.24
  2.3 6.9 %abs_reduce_fusion = (f32[]{:T(128)}, f32[128,8,1792]{2,0,1:T(8,128)}) fusion(bf16[8,128,1792]{2,1,0:T(8,128)(2,1)} %bitcast.132), kind=kOutput, calls=%fused_computation.6 | convolution fusion | flops 475856896 | bytes 11010052 | tf_op jit(solution)/shard_map/kl,bkc->blc/dot_general | solution.py:49
  9.2 1.3 compare_select_fusion.1
  10.5 4.8 %abs_reduce_fusion.1 = (f32[]{:T(128)}, f32[128,8,1792]{2,0,1:T(8,128)}) fusion(bf16[8,128,1792]{2,1,0:T(8,128)(2,1)S(1)} %bitcast.133), kind=kOutput, calls=%fused_computation.7 | convolution fusion | flops 475856896 | bytes 11010052 | tf_op jit(solution)/shard_map/kl,bkc->blc/dot_general | solution.py:49
  15.3 4.7 %abs_reduce_fusion.2 = (f32[]{:T(128)}, f32[64,28,1024]{2,0,1:T(8,128)}) fusion(bf16[28,64,1024]{2,1,0:T(8,128)(2,1)S(1)} %bitcast.134), kind=kOutput, calls=%fused_computation.8 | convolution fusion | flops 240521216 | bytes 11010052 | tf_op jit(solution)/shard_map/kl,bkc->blc/dot_general | solution.py:49
  19.9 2.0 %select_select_fusion.refs_2_ = f32[8,128]{1,0:T(8,128)} fusion(f32[8]{0:T(128)S(1)} %compare_select_fusion.1, f32[]{:T(128)} %get-tuple-element.48, f32[]{:T(128)} %get-tuple-element.50, pred[8]{0:T(512)(128)(4,1)S(1)} %get-tuple-element.52, pred[8]{0:T(512)(128)(4,1)S(1)} %get-tuple-element.53), kind=kLoop, calls=%fused_computation.79 | loop fusion | flops 2048 | bytes 4152 | tf_op jit(solution)/shard_map/jit(_where)/select_n | solution.py:281
  21.9 24.4 %shard_map.92 = (bf16[8,32,1024]{2,1,0:T(8,128)(2,1)}, bf16[8,32,1024]{2,1,0:T(8,128)(2,1)}, f32[4,8,128]{2,1,0:T(8,128)}) custom-call(bf16[32,1024]{1,0:T(8,128)(2,1)} %refs_0_.1, bf16[32,1024]{1,0:T(8,128)(2,1)} %refs_1_.1, f32[8,128]{1,0:T(8,128)} %select_select_fusion.refs_2_), custom_call_target="tpu_custom_call" | custom-call | tf_op jit(solution)/shard_map/pallas_call | solution.py:260
  46.3 1.3 copy.49
  47.6 2.0 %fusion.137 = (f32[1,1,1]{2,1,0:T(1,128)}, f32[1,1,1]{2,1,0:T(1,128)}, f32[1,1,1]{2,1,0:T(1,128)}, f32[1,1,1]{2,1,0:T(1,128)}, f32[1,1,1]{2,1,0:T(1,128)}, /*ind...) fusion(f32[4,8,128]{2,1,0:T(8,128)} %get-tuple-element.18), kind=kLoop, calls=%fused_computation.157 | loop fusion | bytes 88 | tf_op jit(solution)/shard_map/slice | solution.py:298
  49.6 7.1 %multiply_convert_fusion.3 = bf16[64,28,1024]{2,0,1:T(8,128)(2,1)} fusion(f32[64,28,1024]{2,0,1:T(8,128)} %get-tuple-element.51, f32[]{:T(128)} %bitcast.17), kind=kLoop, calls=%fused_computation.3 | loop fusion | flops 7340032 | bytes 11010052 | tf_op jit(solution)/shard_map/convert
  56.7 3.5 %multiply_convert_fusion.4 = bf16[128,8,1792]{2,0,1:T(8,128)(2,1)} fusion(f32[128,8,1792]{2,0,1:T(8,128)S(1)} %bitcast.127, f32[]{:T(128)} %bitcast.12), kind=kLoop, calls=%fused_computation.4 | loop fusion | flops 7340032 | bytes 11010052 | tf_op jit(solution)/shard_map/convert.1
  60.2 3.7 %multiply_convert_fusion.5 = bf16[128,8,1792]{2,0,1:T(8,128)(2,1)} fusion(f32[128,8,1792]{2,0,1:T(8,128)S(1)} %bitcast.125, f32[]{:T(128)} %bitcast.8), kind=kLoop, calls=%fused_computation.5 | loop fusion | flops 7340032 | bytes 11010052 | tf_op jit(solution)/shard_map/convert.2
  66.1 4.5 %fusion.139.refs_1_ = f32[4,64,1792]{2,1,0:T(8,128)} fusion(bf16[4,64,1024]{2,1,0:T(8,128)(2,1)S(1)} %convert_element_type.141, bf16[1024,1792,1]{1,0,2:T(8,128)(2,1)} %bitcast.128), kind=kOutput, calls=%fused_computation.159 | convolution fusion | flops 939524096 | bytes 6029312 | tf_op jit(solution)/shard_map/dot_general | solution.py:316
  70.6 2.4 %fusion.138.refs_0_ = f32[4,64,1792]{2,1,0:T(8,128)} fusion(bf16[4,64,1024]{2,1,0:T(8,128)(2,1)S(1)} %convert_element_type.141, bf16[1024,1792,1]{1,0,2:T(8,128)(2,1)S(1)} %bitcast.130), kind=kOutput, calls=%fused_computation.158 | convolution fusion | flops 939524096 | bytes 6029312 | tf_op jit(solution)/shard_map/dot_general | solution.py:315
  73.0 2.5 %fusion.140.refs_2_ = f32[4,64,1792]{2,1,0:T(8,128)} fusion(bf16[4,64,1024]{2,1,0:T(8,128)(2,1)S(1)} %bitcast.151, bf16[1792,1024,1]{1,0,2:T(8,128)(2,1)S(1)} %bitcast.135), kind=kOutput, calls=%fused_computation.160 | convolution fusion | flops 939524096 | bytes 6029312 | tf_op jit(solution)/shard_map/dot_general | solution.py:70
  75.5 23.7 %shard_map.93 = (f32[64,1792]{1,0:T(8,128)}, f32[64,1792]{1,0:T(8,128)}, f32[64,1792]{1,0:T(8,128)}) custom-call(f32[4,64,1792]{2,1,0:T(8,128)} %fusion.138.refs_0_, f32[4,64,1792]{2,1,0:T(8,128)} %fusion.139.refs_1_, f32[4,64,1792]{2,1,0:T(8,128)} %fusion.140.refs_2_), custom_call_target="tpu_custom_call" | custom-call | tf_op jit(solution)/shard_map/pallas_call | solution.py:185
  99.2 1.8 broadcast_multiply_fusion
  101.4 1.5 convolution_multiply_fusion.4
  103.8 2.3 %multiply_convert_fusion.8 = (bf16[64,1792]{1,0:T(8,128)(2,1)}, bf16[64,1792]{1,0:T(8,128)(2,1)}, bf16[64,1792]{1,0:T(8,128)(2,1)S(1)}) fusion(f32[64,1792]{1,0:T(8,128)S(1)} %mul.246, f32[64,1792]{1,0:T(8,128)S(1)} %copy-done.8, f32[]{:T(128)} %bitcast.21, f32[64,1792]{1,0:T(8,128)S(1)} %copy-done.9, f32[]{:T(128)} %bitcast.22), kind=kLoop, calls=%fused_computation.40 | loop fusion | flops 2064384 | bytes 2064392 | tf_op jit(solution)/shard_map/convert_element_type | solution.py:330
  107.7 1.3 compare_select_fusion
  109.7 26.4 %shard_map.94 = (bf16[4,64,1792]{2,1,0:T(8,128)(2,1)}, bf16[4,64,1792]{2,1,0:T(8,128)(2,1)}, bf16[4,64,1792]{2,1,0:T(8,128)(2,1)}, f32[4,8,128]{2,1,0:T(8,128)}) custom-call(bf16[64,1792]{1,0:T(8,128)(2,1)} %copy-done.6, bf16[64,1792]{1,0:T(8,128)(2,1)} %get-tuple-element.30.refs_1_, bf16[64,1792]{1,0:T(8,128)(2,1)} %get-tuple-element.29.refs_2_, ...), custom_call_target="tpu_custom_call" | custom-call | tf_op jit(solution)/shard_map/pallas_call | solution.py:260
  136.1 4.7 %convolution_multiply_fusion = f32[256,1024]{1,0:T(8,128)S(1)} fusion(bf16[256,1792]{1,0:T(8,128)(2,1)} %bitcast.147, bf16[1024,1792]{1,0:T(8,128)(2,1)} %bitcast.129, f32[]{:T(128)} %bitcast.35), kind=kOutput, calls=%fused_computation.16 | convolution fusion | flops 939786240 | bytes 5636100 | tf_op jit(solution)/shard_map/dot_general | solution.py:70
  140.9 2.7 %fusion.15 = bf16[256,1024]{1,0:T(8,128)(2,1)} fusion(f32[256,1024]{1,0:T(8,128)S(1)} %convolution_multiply_fusion, bf16[256,1792]{1,0:T(8,128)(2,1)S(1)} %bitcast.149, bf16[1024,1792]{1,0:T(8,128)(2,1)S(1)} %bitcast.131, f32[]{:T(128)} %bitcast.32), kind=kOutput, calls=%fused_computation.28 | convolution fusion | flops 940310528 | bytes 6160388 | tf_op jit(solution)/shard_map/dot_general | solution.py:70
  143.5 1.2 fusion.136
  144.7 2.0 %reshape.108 = bf16[256,28,64]{2,1,0:T(8,128)(2,1)S(1)} reshape(bf16[4,64,1792]{2,1,0:T(8,128)(2,1)S(1)} %copy-done.7) | data formatting | bytes 1835008 | tf_op jit(solution)/shard_map/reshape;reshape | solution.py:35
  146.8 2.0 %multiply_convert_fusion.7 = bf16[256,28,64]{0,2,1:T(8,128)(2,1)S(1)} fusion(bf16[256,28,64]{2,1,0:T(8,128)(2,1)S(1)} %reshape.108, f32[]{:T(128)} %bitcast.27), kind=kOutput, calls=%fused_computation.14 | convolution fusion | flops 60690432 | bytes 1835012 | tf_op jit(solution)/shard_map/rbk,kl->rbl/dot_general | solution.py:37
  148.8 1.9 %fusion.17 = bf16[256,1024]{1,0:T(8,128)(2,1)} fusion(bf16[256,28,64]{0,2,1:T(8,128)(2,1)S(1)} %multiply_convert_fusion.7, bf16[64,28,1024]{2,0,1:T(8,128)(2,1)S(1)} %copy-done.5), kind=kOutput, calls=%fused_computation.30 | convolution fusion | flops 939786240 | bytes 5111808 | tf_op jit(solution)/shard_map/dot_general | solution.py:339
  151.2 20.7 %shard_map.95 = (f32[32,1024]{1,0:T(8,128)}, f32[32,1024]{1,0:T(8,128)}) custom-call(bf16[8,32,1024]{2,1,0:T(8,128)(2,1)} %bitcast.141, bf16[8,32,1024]{2,1,0:T(8,128)(2,1)} %bitcast.140), custom_call_target="tpu_custom_call" | custom-call | tf_op jit(solution)/shard_map/pallas_call | solution.py:185
  171.8 2.2 %multiply_convert_fusion.11 = bf16[32,1024]{1,0:T(8,128)(2,1)} fusion(f32[32,1024]{1,0:T(8,128)} %get-tuple-element.27, f32[]{:T(128)} %bitcast.37), kind=kLoop, calls=%fused_computation.45 | loop fusion | flops 65536 | bytes 196612 | tf_op jit(solution)/shard_map/convert_element_type | solution.py:348
  175.9 3.6 %multiply_convert_fusion = bf16[1792,1024]{1,0:T(8,128)(2,1)} fusion(bf16[256,1792]{0,1:T(8,128)(2,1)S(1)} %bitcast.136, bf16[256,1024]{1,0:T(8,128)(2,1)S(1)} %bitcast.152, f32[]{:T(128)} %bitcast.43), kind=kOutput, calls=%fused_computation | convolution fusion | flops 943194112 | bytes 5111812 | tf_op jit(solution)/shard_map/dot_general | solution.py:64
  179.6 3.7 %multiply_convert_fusion.2 = bf16[1024,1792]{1,0:T(8,128)(2,1)} fusion(bf16[256,1024]{0,1:T(8,128)(2,1)S(1)} %bitcast.137, bf16[256,1792]{1,0:T(8,128)(2,1)S(1)} %bitcast.150, f32[]{:T(128)} %bitcast.40), kind=kOutput, calls=%fused_computation.2 | convolution fusion | flops 943194112 | bytes 5111812 | tf_op jit(solution)/shard_map/dot_general | solution.py:64
  183.2 3.6 %multiply_convert_fusion.1 = bf16[1024,1792]{1,0:T(8,128)(2,1)} fusion(bf16[256,1024]{0,1:T(8,128)(2,1)S(1)} %bitcast.138, bf16[256,1792]{1,0:T(8,128)(2,1)S(1)} %bitcast.148, f32[]{:T(128)} %bitcast.40), kind=kOutput, calls=%fused_computation.1 | convolution fusion | flops 943194112 | bytes 5111812 | tf_op jit(solution)/shard_map/dot_general | solution.py:64
  (56 shorter events, 8.2 us)
Async XLA Ops:
  2.3 8.2 %copy-start.2 = (bf16[1024,1792]{1,0:T(8,128)(2,1)S(1)}, bf16[1024,1792]{1,0:T(8,128)(2,1)}, u32[]{:S(2)}) copy-start(bf16[1024,1792]{1,0:T(8,128)(2,1)} %param.8) | copy-start | bytes 11010052
  10.5 4.8 %copy-start.3 = (bf16[1792,1024]{1,0:T(8,128)(2,1)S(1)}, bf16[1792,1024]{1,0:T(8,128)(2,1)}, u32[]{:S(2)}) copy-start(bf16[1792,1024]{1,0:T(8,128)(2,1)} %param.9) | copy-start | bytes 11010052
  15.3 41.4 %slice-start.2 = ((s8[7340032]{0:T(1024)(128)(4,1)}), s8[3145728]{0:T(1024)(128)(4,1)S(1)}, s32[]{:S(2)}) async-start(s8[7340032]{0:T(1024)(128)(4,1)} %bitcast.126), calls=%async_computation.2 | async-start | bytes 6291456
  46.3 10.4 %slice-start.3 = ((s8[7340032]{0:T(1024)(128)(4,1)}), s8[4194304]{0:T(1024)(128)(4,1)S(1)}, s32[]{:S(2)}) async-start(s8[7340032]{0:T(1024)(128)(4,1)} %bitcast.126), calls=%async_computation.3 | async-start | bytes 8388608
  46.3 13.9 %slice-start = ((s8[7340032]{0:T(1024)(128)(4,1)}), s8[4194304]{0:T(1024)(128)(4,1)S(1)}, s32[]{:S(2)}) async-start(s8[7340032]{0:T(1024)(128)(4,1)} %bitcast.124), calls=%async_computation | async-start | bytes 8388608
  49.6 10.6 %slice-start.1 = ((s8[7340032]{0:T(1024)(128)(4,1)}), s8[3145728]{0:T(1024)(128)(4,1)S(1)}, s32[]{:S(2)}) async-start(s8[7340032]{0:T(1024)(128)(4,1)} %bitcast.124), calls=%async_computation.1 | async-start | bytes 6291456
  66.1 4.5 %copy-start = (bf16[128,8,1792]{2,0,1:T(8,128)(2,1)S(1)}, bf16[128,8,1792]{2,0,1:T(8,128)(2,1)}, u32[]{:S(2)}) copy-start(bf16[128,8,1792]{2,0,1:T(8,128)(2,1)} %multiply_convert_fusion.5) | copy-start | bytes 11010052
  70.6 2.4 %copy-start.4 = (bf16[64,28,1024]{2,0,1:T(8,128)(2,1)S(1)}, bf16[64,28,1024]{2,0,1:T(8,128)(2,1)}, u32[]{:S(2)}) copy-start(bf16[64,28,1024]{2,0,1:T(8,128)(2,1)} %multiply_convert_fusion.3) | copy-start | bytes 11010052
  70.6 2.4 %copy-start.13 = (bf16[8,32,1024]{2,1,0:T(8,128)(2,1)S(1)}, bf16[8,32,1024]{2,1,0:T(8,128)(2,1)}, u32[]{:S(2)}) copy-start(bf16[8,32,1024]{2,1,0:T(8,128)(2,1)} %get-tuple-element.19) | copy-start | bytes 1572868
  99.2 4.6 %copy-start.8 = (f32[64,1792]{1,0:T(8,128)S(1)}, f32[64,1792]{1,0:T(8,128)}, u32[]{:S(2)}) copy-start(f32[64,1792]{1,0:T(8,128)} %get-tuple-element.20) | copy-start | bytes 1376260
  99.2 4.6 %copy-start.9 = (f32[64,1792]{1,0:T(8,128)S(1)}, f32[64,1792]{1,0:T(8,128)}, u32[]{:S(2)}) copy-start(f32[64,1792]{1,0:T(8,128)} %get-tuple-element.21) | copy-start | bytes 1376260
  106.1 3.6 %copy-start.6 = (bf16[64,1792]{1,0:T(8,128)(2,1)}, bf16[64,1792]{1,0:T(8,128)(2,1)S(1)}, u32[]{:S(2)}) copy-start(bf16[64,1792]{1,0:T(8,128)(2,1)S(1)} %get-tuple-element.31.refs_0_) | copy-start | bytes 688132
  136.1 4.7 %copy-start.1 = (bf16[128,8,1792]{2,0,1:T(8,128)(2,1)S(1)}, bf16[128,8,1792]{2,0,1:T(8,128)(2,1)}, u32[]{:S(2)}) copy-start(bf16[128,8,1792]{2,0,1:T(8,128)(2,1)} %multiply_convert_fusion.5) | copy-start | bytes 11010052
  136.1 4.7 %copy-start.11 = (bf16[4,64,1792]{2,1,0:T(8,128)(2,1)S(1)}, bf16[4,64,1792]{2,1,0:T(8,128)(2,1)}, u32[]{:S(2)}) copy-start(bf16[4,64,1792]{2,1,0:T(8,128)(2,1)} %get-tuple-element.25) | copy-start | bytes 2752516
  140.8 3.9 %copy-start.7 = (bf16[4,64,1792]{2,1,0:T(8,128)(2,1)S(1)}, bf16[4,64,1792]{2,1,0:T(8,128)(2,1)}, u32[]{:S(2)}) copy-start(bf16[4,64,1792]{2,1,0:T(8,128)(2,1)} %get-tuple-element.23) | copy-start | bytes 2752516
  146.7 2.1 %copy-start.5 = (bf16[64,28,1024]{2,0,1:T(8,128)(2,1)S(1)}, bf16[64,28,1024]{2,0,1:T(8,128)(2,1)}, u32[]{:S(2)}) copy-start(bf16[64,28,1024]{2,0,1:T(8,128)(2,1)} %multiply_convert_fusion.3) | copy-start | bytes 11010052
  150.7 25.2 %copy-start.14 = (bf16[8,32,1024]{2,1,0:T(8,128)(2,1)S(1)}, bf16[8,32,1024]{2,1,0:T(8,128)(2,1)}, u32[]{:S(2)}) copy-start(bf16[8,32,1024]{2,1,0:T(8,128)(2,1)} %get-tuple-element.19) | copy-start | bytes 1572868
  175.9 3.6 %copy-start.12 = (bf16[4,64,1792]{2,1,0:T(8,128)(2,1)S(1)}, bf16[4,64,1792]{2,1,0:T(8,128)(2,1)}, u32[]{:S(2)}) copy-start(bf16[4,64,1792]{2,1,0:T(8,128)(2,1)} %get-tuple-element.25) | copy-start | bytes 2752516
  179.6 3.7 %copy-start.10 = (bf16[4,64,1792]{2,1,0:T(8,128)(2,1)S(1)}, bf16[4,64,1792]{2,1,0:T(8,128)(2,1)}, u32[]{:S(2)}) copy-start(bf16[4,64,1792]{2,1,0:T(8,128)(2,1)} %get-tuple-element.26) | copy-start | bytes 2752516
